TPU v7x, 32 devices: a whole 2x2x4 slice. The times are simulated.
32 devices in a mesh: dp: 8 (over z, y), comp: 4 (over x, core).
Axes of the slice: x: 2, y: 2, z: 4, core: 2. Of those that a mesh axis runs over, the one named last changes fastest.
Arguments:
- points: float32 [8192, 128], P('dp'), may hold values from -64 to 64
- block_counts: int32 [8], replicated, may hold values from 1 to 16, as said below
- block_dest: int32 [8, 16], replicated, may hold values from 0 to 7, as said below
- means: float32 [256, 128], P(('dp', 'comp')), may hold values from -3 to 3
- factors: float32 [256, 128, 128], P(('dp', 'comp')), may hold values from -0.25 to 1.4, as said below
- log_weights: float32 [256], P(('dp', 'comp')), may hold values from -4 to 4
Outputs:
- new_means: float32 [256, 128], P(('dp', 'comp'))
- new_factors: float32 [256, 128, 128], P(('dp', 'comp'))
- new_log_weights: float32 [256], P(('dp', 'comp'))
- log_density: float32 [2048], P('dp')
Inputs may be any that keep to these rules, and one draw needn't show every extreme that they name: `block_counts`: blocks live on each index of dp on entry; they sum to 32, and one index holds exactly 16. `block_dest`: for j < block_counts[s], the index of dp that receives block j of index s; every index receives exactly 4 blocks, no index sends more than 2 blocks to one index, and some index sends exactly 2 to one; entries with j >= block_counts[s] are unused. `factors`: each matrix is upper triangular with diagonal entries from 0.7 to 1.4.
All inputs are finite; a program needn't handle non-finite values.
Results may differ from a plain program's by a relative error of at most 0.003.
Values sent between devices are 32-bit elements; how exact they have to be, the bound alone decides.
A program may use at most 128 MiB of HBM per device.

v0:
```python
import math

import jax
import jax.numpy as jnp
from jax import lax
from jax.experimental import pallas as pl
from jax.experimental.pallas import tpu as pltpu
from jax.sharding import PartitionSpec as P

ITERS = 2

density_precision = lax.Precision.HIGHEST
moment_precision = lax.Precision.HIGHEST
log_two_pi = math.log(2.0 * math.pi)
PARAMS = pltpu.CompilerParams(vmem_limit_bytes=56 * 1024 * 1024)
VMEM = pl.BlockSpec(memory_space=pltpu.VMEM)
SMEM = pl.BlockSpec(memory_space=pltpu.SMEM)
PANEL = 8


def pack_kernel(me_ref, counts_ref, dest_ref, points_ref, out_ref, fill_ref):
    devices = counts_ref.shape[0]
    slots = out_ref.shape[0] // devices
    me = me_ref[0]

    def clear(e, carry):
        fill_ref[e] = 0
        return carry

    lax.fori_loop(0, devices, clear, 0)

    def move(j, carry):
        e = dest_ref[me, j]
        slot = fill_ref[e]
        fill_ref[e] = slot + 1
        out_ref[e * slots + slot] = points_ref[j]
        return carry

    lax.fori_loop(0, counts_ref[me], move, 0)


def order_kernel(me_ref, counts_ref, dest_ref, in_ref, out_ref):
    devices = counts_ref.shape[0]
    slots = in_ref.shape[0] // devices
    me = me_ref[0]

    def source(s, place):
        def block(j, state):
            place, slot = state
            hit = dest_ref[s, j] == me

            @pl.when(hit)
            def _():
                out_ref[place] = in_ref[s * slots + slot]

            step = hit.astype(jnp.int32)
            return place + step, slot + step

        return lax.fori_loop(0, counts_ref[s], block, (place, jnp.int32(0)))[0]

    lax.fori_loop(0, devices, source, jnp.int32(0))


def chunk_of(total):
    return math.gcd(total, 1024)


def eye_mask(width):
    rows = lax.broadcasted_iota(jnp.int32, (width, width), 0)
    cols = lax.broadcasted_iota(jnp.int32, (width, width), 1)
    return rows == cols


def density_stage(xt_ref, mu_ref, p_ref, w_ref, table_ref, lse_ref):
    width, total = xt_ref.shape
    members = p_ref.shape[0]
    chunk = chunk_of(total)
    diagonal = eye_mask(width)

    def member(b, carry):
        factor = p_ref[b]
        diag = jnp.sum(jnp.where(diagonal, factor, 0.0), axis=0, keepdims=True)
        logdet = jnp.sum(jnp.log(diag), axis=1, keepdims=True)
        offset = w_ref[b] + logdet - 0.5 * width * log_two_pi
        centre = mu_ref[b]
        factor_t = factor.T

        def piece(c, carry):
            cols = pl.ds(pl.multiple_of(c * chunk, chunk), chunk)
            z = xt_ref[:, cols] - centre
            y = jnp.dot(
                factor_t, z, precision=density_precision, preferred_element_type=jnp.float32
            )
            table_ref[b, :, cols] = offset - 0.5 * jnp.sum(y * y, axis=0, keepdims=True)
            return carry

        return lax.fori_loop(0, total // chunk, piece, carry)

    lax.fori_loop(0, members, member, 0)

    table = table_ref[...]
    peak = jnp.max(table, axis=0)
    lse_ref[...] = peak + jnp.log(jnp.sum(jnp.exp(table - peak[None]), axis=0))


def eliminate(m_ref, l_ref, width):
    lane = lax.broadcasted_iota(jnp.int32, (8, width), 1)

    def spread(v, j):
        return jnp.take_along_axis(v, jnp.full((8, width), j, jnp.int32), axis=1)

    def row(j):
        return pl.ds(pl.multiple_of(j * 8, 8), 8)

    def ready(value, j):
        pivot = spread(value, j)
        ahead = spread(value, jnp.minimum(j + 1, width - 1))
        scaled = jnp.where(lane == j, 1.0, value) * (1.0 / pivot)
        kept = jnp.where(lane < j, value, jnp.where(lane == j, 1.0, 0.0))
        root = lax.rsqrt(pivot)
        root = root * (1.5 - 0.5 * pivot * root * root)
        l_ref[row(j), :] = kept * root
        return scaled, ahead

    state = ready(m_ref[row(0), :], 0)
    for start in range(0, width, PANEL):

        def pivot_step(j, state, start=start):
            scaled, ahead = state
            here = lane == j
            following = jnp.where(here, 0.0, m_ref[row(j + 1), :]) - ahead * scaled
            for i in range(start + 2, width):
                old = m_ref[i * 8 : i * 8 + 8, :]
                new = jnp.where(here, 0.0, old) - spread(old, j) * scaled
                if i < start + PANEL + 1:
                    new = jnp.where(jnp.full((8, width), i, jnp.int32) > j + 1, new, old)
                m_ref[i * 8 : i * 8 + 8, :] = new
            return ready(following, j + 1)

        state = lax.fori_loop(start, min(start + PANEL, width - 1), pivot_step, state)


def update_stage(
    total_points, xt_ref, table_ref, all_ref, mu_ref,
    new_mu_ref, new_p_ref, new_w_ref, total_ref, resp_ref, m_ref, l_ref,
):
    width, total = xt_ref.shape
    members = mu_ref.shape[0]
    chunk = chunk_of(total)
    lses = all_ref[...]
    peak = jnp.max(lses, axis=0)
    log_total = peak + jnp.log(jnp.sum(jnp.exp(lses - peak[None]), axis=0))
    total_ref[...] = log_total
    resp_ref[...] = jnp.exp(table_ref[...] - log_total[None])
    diagonal = eye_mask(width)
    identity = jnp.where(diagonal, 1.0, 0.0)

    def batch(b):
        return pl.ds(b, width, stride=8)

    for b in range(members, 8):
        m_ref[batch(b), :] = identity

    def member(b, carry):
        centre = mu_ref[b]

        def piece(c, sums):
            second, first = sums
            cols = pl.ds(pl.multiple_of(c * chunk, chunk), chunk)
            z = xt_ref[:, cols] - centre
            weighted = z * resp_ref[b, :, cols]
            second += lax.dot_general(
                weighted, z, (((1,), (1,)), ((), ())),
                precision=moment_precision, preferred_element_type=jnp.float32,
            )
            return second, first + jnp.sum(weighted, axis=1, keepdims=True)

        second, first = lax.fori_loop(
            0, total // chunk, piece,
            (jnp.zeros((width, width), jnp.float32), jnp.zeros((width, 1), jnp.float32)),
        )
        counted = jnp.sum(resp_ref[b], axis=1, keepdims=True) + 1.0
        column = jnp.broadcast_to(first, (width, width))
        covariance = (second - column * column.T / counted + identity) / counted
        m_ref[batch(b), :] = covariance
        new_mu_ref[b] = centre + first / counted
        new_w_ref[b] = jnp.log(counted / total_points)
        return carry

    lax.fori_loop(0, members, member, 0)
    eliminate(m_ref, l_ref, width)

    def emit(b, carry):
        new_p_ref[b] = l_ref[batch(b), :].T
        return carry

    lax.fori_loop(0, members, emit, 0)


def first_kernel(x_ref, mu_ref, p_ref, w_ref, xt_ref, table_ref, lse_ref):
    total, width = x_ref.shape
    chunk = math.gcd(total, 512)

    def flip(c, carry):
        at = pl.ds(pl.multiple_of(c * chunk, chunk), chunk)
        xt_ref[:, at] = x_ref[at, :].T
        return carry

    lax.fori_loop(0, total // chunk, flip, 0)
    density_stage(xt_ref, mu_ref, p_ref, w_ref, table_ref, lse_ref)


def middle_kernel(
    total_points, xt_ref, table_ref, all_ref, mu_ref,
    new_mu_ref, new_p_ref, new_w_ref, new_table_ref, lse_ref,
    total_ref, resp_ref, m_ref, l_ref,
):
    update_stage(
        total_points, xt_ref, table_ref, all_ref, mu_ref,
        new_mu_ref, new_p_ref, new_w_ref, total_ref, resp_ref, m_ref, l_ref,
    )
    density_stage(xt_ref, new_mu_ref, new_p_ref, new_w_ref, new_table_ref, lse_ref)


def last_kernel(total_points, *refs):
    update_stage(total_points, *refs)


def f32(*shape):
    return jax.ShapeDtypeStruct(shape, jnp.float32)


def call(kernel, out_shape, *args, scratch=(), specs=None):
    return pl.pallas_call(
        kernel,
        out_shape=out_shape,
        in_specs=specs or [VMEM] * len(args),
        out_specs=jax.tree.map(lambda _: VMEM, out_shape),
        scratch_shapes=list(scratch),
        compiler_params=PARAMS,
    )(*args)


def gather_live(points, block_counts, block_dest):
    devices = lax.axis_size("dp")
    nblocks = block_dest.shape[1]
    width = points.shape[1]
    rows = points.shape[0] // nblocks
    slots = (nblocks + devices - 1) // devices
    me = lax.axis_index("dp").astype(jnp.int32).reshape(1)
    specs = [SMEM, SMEM, SMEM, VMEM]
    outgoing = call(
        pack_kernel, f32(devices * slots, rows, width),
        me, block_counts, block_dest, points.reshape(nblocks, rows, width),
        specs=specs, scratch=[pltpu.SMEM((devices,), jnp.int32)],
    )
    incoming = lax.all_to_all(outgoing, "dp", split_axis=0, concat_axis=0, tiled=True)
    live = call(
        order_kernel, f32(RB, rows, width), me, block_counts, block_dest, incoming, specs=specs
    )
    return live.reshape(RB * rows, width)


RB = 4


def exchange(lse):
    return lax.all_gather(lse, ("dp", "comp"))


def per_device(points, block_counts, block_dest, means, factors, log_weights):
    members, width = means.shape
    mine = gather_live(points, block_counts, block_dest)
    x = lax.all_gather(mine, "dp", axis=0, tiled=True)
    total = x.shape[0]
    total_points = float(total + members * lax.axis_size("dp") * lax.axis_size("comp"))
    mu = means.reshape(members, width, 1)
    weights = log_weights.reshape(members, 1, 1)
    factor = factors
    xt, table, lse = call(
        first_kernel, (f32(width, total), f32(members, 1, total), f32(1, total)),
        x, mu, factor, weights,
    )
    scratch = [
        pltpu.VMEM((members, 1, total), jnp.float32),
        pltpu.VMEM((width * 8, width), jnp.float32),
        pltpu.VMEM((width * 8, width), jnp.float32),
    ]
    params = (f32(members, width, 1), f32(members, width, width), f32(members, 1, 1))
    for iteration in range(ITERS):
        gathered = exchange(lse)
        if iteration < ITERS - 1:
            mu, factor, weights, table, lse = call(
                lambda *refs: middle_kernel(total_points, *refs),
                params + (f32(members, 1, total), f32(1, total)),
                xt, table, gathered, mu,
                scratch=[pltpu.VMEM((1, total), jnp.float32)] + scratch,
            )
        else:
            mu, factor, weights, log_total = call(
                lambda *refs: last_kernel(total_points, *refs),
                params + (f32(1, total),),
                xt, table, gathered, mu, scratch=scratch,
            )
    share = total // lax.axis_size("dp")
    own = lax.dynamic_slice_in_dim(log_total.reshape(total), lax.axis_index("dp") * share, share)
    return (mu.reshape(members, width), factor, weights.reshape(members), own / width)


def solution(mesh):
    in_specs = (
        P("dp", None),
        P(),
        P(),
        P(("dp", "comp"), None),
        P(("dp", "comp"), None, None),
        P(("dp", "comp")),
    )
    out_specs = (P(("dp", "comp"), None), P(("dp", "comp"), None, None), P(("dp", "comp")), P("dp"))
    return jax.shard_map(
        per_device, mesh=mesh, in_specs=in_specs, out_specs=out_specs, check_vma=False
    )
```

profile of v0, /device:TPU:0, one launch (start us, length us, event | category | flops | bytes accessed | tf_op | source)
XLA Modules:
  0.0 265.0 jit_solution(14443765968064202629)
XLA Ops:
  7.2 0.0 all-gather.6.cloned.1.call-start
  7.2 1.9 shard_map.93
  9.1 22.0 %all_to_all.5.in_ref = f32[16,64,128]{2,1,0:T(8,128)} all-to-all(f32[16,64,128]{2,1,0:T(8,128)} %shard_map.93), channel_id=1, replica_groups=mesh['dp'=8,'comp'=4] {'dp'}, dimensions={0} | all-to-all | bytes 1048576 | tf_op jit(solution)/shard_map/all_to_all | solution.py:257
  31.1 2.3 shard_map.94
  33.4 0.0 copy-start.2
  33.4 0.0 all-gather.6.cloned.1.call-update
  33.4 0.0 copy-start
  33.5 0.6 copy-done.2
  34.1 0.7 copy.15.w_ref
  34.7 0.0 copy-done
  34.7 1.0 copy.14.mu_ref.refs_3_
  35.8 37.1 %all-gather.6.cloned.1.call-done.x_ref = f32[2048,128]{1,0:T(8,128)} async-done(((f32[256,128]{1,0:T(8,128)}), f32[2048,128]{1,0:T(8,128)}) %all-gather.6.cloned.1.call-update) | async-done | bytes 1048592 | tf_op jit(solution)/shard_map/all_gather | solution.py:274
  72.9 15.4 %shard_map.95 = (f32[128,2048]{1,0:T(8,128)}, f32[8,1,2048]{2,1,0:T(1,128)}, f32[1,2048]{1,0:T(1,128)}) custom-call(f32[2048,128]{1,0:T(8,128)} %all-gather.6.cloned.1.call-done.x_ref, f32[8,128,1]{2,1,0:T(8,128)} %copy.14.mu_ref.refs_3_, f32[8,128,128]{2,1,0:T(8,128)} %p_ref.1, f32[8,1,1]{2,1,0:T(1,128)} %copy.15.w_ref), custom_call_target="tpu_custom_call" | custom-call | tf_op jit(solution)/shard_map/pallas_call | solution.py:234
  88.3 42.8 %all-gather.2.refs_2_ = f32[32,1,2048]{2,1,0:T(1,128)} all-gather(f32[1,1,2048]{2,1,0:T(1,128)} %bitcast.11), channel_id=2, replica_groups=mesh['dp'=8,'comp'=4] {'dp','comp'}, dimensions={0}, use_global_device_ids=true | all-gather | bytes 270336 | tf_op jit(solution)/shard_map/all_gather | solution.py:268
  131.1 47.9 %shard_map.96 = (f32[8,128,1]{2,1,0:T(8,128)}, f32[8,128,128]{2,1,0:T(8,128)}, f32[8,1,1]{2,1,0:T(1,128)}, f32[8,1,2048]{2,1,0:T(1,128)}, f32[1,2048]{1,0:T(1,128)}) custom-call(f32[128,2048]{1,0:T(8,128)} %get-tuple-element.14.refs_0_, f32[8,1,2048]{2,1,0:T(1,128)} %get-tuple-element.15.refs_1_, f32[32,1,2048]{2,1,0:T(1,128)} %all-gather.2.refs_2_, ...), custom_call_target="tpu_custom_call" | custom-call | tf_op jit(solution)/shard_map/pallas_call | solution.py:234
  179.0 40.2 %all-gather.3.refs_2_ = f32[32,1,2048]{2,1,0:T(1,128)} all-gather(f32[1,1,2048]{2,1,0:T(1,128)} %bitcast.10), channel_id=3, replica_groups=mesh['dp'=8,'comp'=4] {'dp','comp'}, dimensions={0}, use_global_device_ids=true | all-gather | bytes 270336 | tf_op jit(solution)/shard_map/all_gather | solution.py:268
  219.2 35.3 %shard_map.97 = (f32[8,128,1]{2,1,0:T(8,128)}, f32[8,128,128]{2,1,0:T(8,128)}, f32[8,1,1]{2,1,0:T(1,128)}, f32[1,2048]{1,0:T(1,128)}) custom-call(f32[128,2048]{1,0:T(8,128)} %get-tuple-element.14.refs_0_, f32[8,1,2048]{2,1,0:T(1,128)} %get-tuple-element.17.refs_1_, f32[32,1,2048]{2,1,0:T(1,128)} %all-gather.3.refs_2_, f32[8,128,1]{2,1,0:T(8,128)} %get-tuple-element.19.refs_3_), custom_call_target="tpu_custom_call" | custom-call | tf_op jit(solution)/shard_map/pallas_call | solution.py:234
  254.5 0.0 copy-start.1
  254.5 1.8 reduce
  256.3 0.0 copy-done.1
  256.3 0.7 reduce.1
  257.0 1.2 dynamic-slice_multiply_fusion
Async XLA Ops:
  7.2 65.7 %all-gather.6.cloned.1.call-start = ((), (), s32[]{:S(2)}) async-start(), calls=%async_computation.1 | async-start | bytes 1179648 | tf_op jit(solution)/shard_map/all_gather | solution.py:274
  33.4 0.7 copy-start.2
  33.4 1.3 copy-start
  254.5 1.9 copy-start.1
Sparse Core Ops, SparseCore 0:
  33.6 39.2 all-gather.5
where the time goes:
time: 265 us
  blocking collectives  105 us (40%)
  Pallas kernels  103 us (39%)
  waiting for transfers between devices  37.1 us (14%)
  between operations  14 us (5%)
  other arithmetic  3.72 us (1%)
    pallas_call x5, Pallas kernels, call(): pl.pallas_call(kernel, out_shape=out_shape, in_specs=specs or [VMEM] * le...  103 us
    all_gather x2, blocking collectives, exchange(): return lax.all_gather(lse, ('dp', 'comp'))  83 us
    all_gather x1, waiting for transfers between devices, per_device(): x = lax.all_gather(mine, 'dp', axis=0, tiled=True)  37.1 us
    all_to_all x1, blocking collectives, gather_live(): lax.all_to_all(outgoing, 'dp', split_axis=0, concat_axis=0, tiled=True)  22 us
  transfers between devices with their start and end apart: 1, of which 1 were waited for; matrix products, arithmetic and copies ran while one was open for 1% of the time, Pallas kernels for 0%

commit v1 on v0

--- a/solution.py
+++ b/solution.py
@@ -15,50 +15,264 @@
 PARAMS = pltpu.CompilerParams(vmem_limit_bytes=56 * 1024 * 1024)
 VMEM = pl.BlockSpec(memory_space=pltpu.VMEM)
 SMEM = pl.BlockSpec(memory_space=pltpu.SMEM)
+ANY = pl.BlockSpec(memory_space=pl.ANY)
 PANEL = 8
 
 
-def pack_kernel(me_ref, counts_ref, dest_ref, points_ref, out_ref, fill_ref):
-    devices = counts_ref.shape[0]
-    slots = out_ref.shape[0] // devices
-    me = me_ref[0]
-
-    def clear(e, carry):
-        fill_ref[e] = 0
-        return carry
-
-    lax.fori_loop(0, devices, clear, 0)
-
-    def move(j, carry):
-        e = dest_ref[me, j]
-        slot = fill_ref[e]
-        fill_ref[e] = slot + 1
-        out_ref[e * slots + slot] = points_ref[j]
-        return carry
-
-    lax.fori_loop(0, counts_ref[me], move, 0)
-
-
-def order_kernel(me_ref, counts_ref, dest_ref, in_ref, out_ref):
-    devices = counts_ref.shape[0]
-    slots = in_ref.shape[0] // devices
-    me = me_ref[0]
-
-    def source(s, place):
-        def block(j, state):
-            place, slot = state
-            hit = dest_ref[s, j] == me
-
-            @pl.when(hit)
-            def _():
-                out_ref[place] = in_ref[s * slots + slot]
-
-            step = hit.astype(jnp.int32)
-            return place + step, slot + step
-
-        return lax.fori_loop(0, counts_ref[s], block, (place, jnp.int32(0)))[0]
-
-    lax.fori_loop(0, devices, source, jnp.int32(0))
+def talking(number):
+    return pltpu.CompilerParams(
+        vmem_limit_bytes=56 * 1024 * 1024, collective_id=number, has_side_effects=True
+    )
+
+
+MESH = pl.DeviceIdType.MESH
+
+
+def here():
+    comps = lax.axis_size("comp")
+    return lax.axis_index("dp") * comps + lax.axis_index("comp")
+
+
+def device(flat):
+    comps = lax.axis_size("comp")
+    return {"dp": flat // comps, "comp": flat % comps}
+
+
+def device_count():
+    return lax.axis_size("dp") * lax.axis_size("comp")
+
+
+def greet():
+    devices = device_count()
+    me = here()
+    barrier = pltpu.get_barrier_semaphore()
+
+    def one(d, carry):
+        pl.semaphore_signal(
+            barrier, inc=1, device_id=device((me + d) % devices), device_id_type=MESH
+        )
+        return carry
+
+    lax.fori_loop(1, devices, one, 0)
+
+
+def greeted():
+    pl.semaphore_wait(pltpu.get_barrier_semaphore(), device_count() - 1)
+
+
+def remote(src, dst, send_sem, recv_sem, where):
+    return pltpu.make_async_remote_copy(
+        src_ref=src, dst_ref=dst, send_sem=send_sem, recv_sem=recv_sem,
+        device_id=where, device_id_type=MESH,
+    )
+
+
+def gather_stage(
+    counts_ref, dest_ref, points_ref, x_ref,
+    part_ref, out_ref, in_ref, mine_ref,
+    load_sem, sent, came, spread_sent, spread_came, pair_sent, pair_came, own_sem,
+):
+    groups = lax.axis_size("dp")
+    comps = lax.axis_size("comp")
+    nblocks, share, width = part_ref.shape
+    slots = out_ref.shape[1]
+    places = mine_ref.shape[0]
+    e = lax.axis_index("dp")
+    c = lax.axis_index("comp")
+
+    load = pltpu.make_async_copy(
+        points_ref.at[:, pl.ds(pl.multiple_of(c * share, share), share), :], part_ref, load_sem
+    )
+    load.start()
+    load.wait()
+    live = counts_ref[e]
+
+    def pack(t, carry):
+        found = jnp.int32(0)
+        at = [jnp.int32(0)] * slots
+        for j in range(nblocks):
+            hit = jnp.logical_and(dest_ref[e, j] == t, j < live)
+            for s in range(slots):
+                at[s] = jnp.where(jnp.logical_and(hit, found == s), j, at[s])
+            found = found + hit.astype(jnp.int32)
+        for s in range(slots):
+            out_ref[t, s] = part_ref[at[s]]
+        return carry
+
+    lax.fori_loop(0, groups, pack, 0)
+    greeted()
+
+    def peer(d):
+        return (e + d) % groups
+
+    def exchange(t, s):
+        return remote(
+            out_ref.at[t], in_ref.at[s], sent.at[t], came.at[s], {"dp": t, "comp": c}
+        )
+
+    def send(d, carry):
+        exchange(peer(d), e).start()
+        return carry
+
+    lax.fori_loop(1, groups, send, 0)
+    in_ref[e] = out_ref[e]
+
+    def locate(s, state):
+        place, froms = state
+        number = counts_ref[s]
+        hits = jnp.int32(0)
+        for j in range(nblocks):
+            hit = jnp.logical_and(dest_ref[s, j] == e, j < number)
+            hits = hits + hit.astype(jnp.int32)
+        froms = list(froms)
+        for q in range(slots):
+            alive = q < hits
+            for p in range(places):
+                froms[p] = jnp.where(jnp.logical_and(alive, place == p), s * slots + q, froms[p])
+            place = place + alive.astype(jnp.int32)
+        return place, tuple(froms)
+
+    _, froms = lax.fori_loop(
+        0, groups, locate, (jnp.int32(0), (jnp.int32(0),) * places)
+    )
+
+    def arrived(d, carry):
+        exchange(peer(d), peer(d)).wait_recv()
+        return carry
+
+    lax.fori_loop(1, groups, arrived, 0)
+    for p in range(places):
+        mine_ref[p] = in_ref[froms[p] // slots, froms[p] % slots]
+
+    def block(owner, column):
+        return x_ref.at[owner, :, column]
+
+    def spread(t, s):
+        return remote(
+            mine_ref, block(s, c), spread_sent.at[t], spread_came.at[s], {"dp": t, "comp": c}
+        )
+
+    def spread_out(d, carry):
+        spread(peer(d), e).start()
+        return carry
+
+    lax.fori_loop(1, groups, spread_out, 0)
+    own = pltpu.make_async_copy(mine_ref, block(e, c), own_sem)
+    own.start()
+
+    bits = [1 << b for b in reversed(range(comps.bit_length() - 1))]
+
+    def hop(level, index, owner, column):
+        src = block(owner, column)
+        return remote(
+            src, src, pair_sent.at[level, index, owner], pair_came.at[level, index, owner],
+            {"dp": e, "comp": c ^ bits[level]},
+        )
+
+    own.wait()
+    columns = [c]
+    for level in range(len(bits)):
+        def forward(d, carry, level=level, columns=tuple(columns)):
+            owner = peer(d)
+            if level == 0:
+                @pl.when(d > 0)
+                def _():
+                    spread(owner, owner).wait_recv()
+            for index, column in enumerate(columns):
+                if level > 0 and index >= len(columns) // 2:
+                    hop(level - 1, index - len(columns) // 2, owner, column).wait_recv()
+                hop(level, index, owner, column).start()
+            return carry
+
+        lax.fori_loop(0, groups, forward, 0)
+        columns = columns + [column ^ bits[level] for column in columns]
+
+    last = len(bits) - 1
+
+    def finish(d, carry):
+        owner = peer(d)
+        for index, column in enumerate(columns[len(columns) // 2:]):
+            hop(last, index, owner, column).wait_recv()
+        for level in range(len(bits)):
+            for index in range(1 << level):
+                hop(level, index, owner, columns[index]).wait_send()
+
+        @pl.when(d > 0)
+        def _():
+            exchange(owner, owner).wait_send()
+            spread(owner, owner).wait_send()
+
+        return carry
+
+    lax.fori_loop(0, groups, finish, 0)
+
+
+def merge_stage(lse_ref, total_ref, near_ref, part_ref, all_ref, near_sems, sent, came):
+    comps = lax.axis_size("comp")
+    devices = device_count()
+    me = here()
+    half = near_ref.shape[1]
+    which = me % 2
+
+    def cut(part):
+        return pl.ds(pl.multiple_of(part * half, half), half)
+
+    near = remote(
+        lse_ref.at[:, cut(1 - which)], near_ref, near_sems.at[0], near_sems.at[1],
+        device(me + 1 - 2 * which),
+    )
+    near.start()
+    near.wait()
+    mine = lse_ref[:, cut(which)]
+    other = near_ref[...]
+    peak = jnp.maximum(mine, other)
+    part = peak + jnp.log(jnp.exp(mine - peak) + jnp.exp(other - peak))
+    part_ref[...] = part
+
+    def row(source):
+        return all_ref.at[source % 2, pl.ds(source // 2, 1)]
+
+    def far(target, source):
+        return remote(part_ref, row(source), sent.at[target], came.at[source], device(target))
+
+    def send(d, carry):
+        far((me + d) % devices, me).start()
+        return carry
+
+    lax.fori_loop(1, devices, send, 0)
+    all_ref[which, pl.ds(me // 2, 1)] = part
+
+    def arrived(d, carry):
+        source = (me + d) % devices
+        far(source, source).wait_recv()
+        return carry
+
+    lax.fori_loop(1, devices, arrived, 0)
+    for h in range(2):
+        values = all_ref[h]
+        peak = jnp.max(values, axis=0, keepdims=True)
+        total_ref[:, h * half : (h + 1) * half] = peak + jnp.log(
+            jnp.sum(jnp.exp(values - peak), axis=0, keepdims=True)
+        )
+
+    def left(d, carry):
+        target = (me + d) % devices
+        far(target, target).wait_send()
+        return carry
+
+    lax.fori_loop(1, devices, left, 0)
+
+
+def merge_scratch(total):
+    devices = device_count()
+    return [
+        pltpu.VMEM((1, total // 2), jnp.float32),
+        pltpu.VMEM((1, total // 2), jnp.float32),
+        pltpu.VMEM((2, devices // 2, total // 2), jnp.float32),
+        pltpu.SemaphoreType.DMA((2,)),
+        pltpu.SemaphoreType.DMA((devices,)),
+        pltpu.SemaphoreType.DMA((devices,)),
+    ]
 
 
 def chunk_of(total):
@@ -141,16 +355,13 @@
 
 
 def update_stage(
-    total_points, xt_ref, table_ref, all_ref, mu_ref,
-    new_mu_ref, new_p_ref, new_w_ref, total_ref, resp_ref, m_ref, l_ref,
+    total_points, xt_ref, table_ref, total_ref, mu_ref,
+    new_mu_ref, new_p_ref, new_w_ref, resp_ref, m_ref, l_ref,
 ):
     width, total = xt_ref.shape
     members = mu_ref.shape[0]
     chunk = chunk_of(total)
-    lses = all_ref[...]
-    peak = jnp.max(lses, axis=0)
-    log_total = peak + jnp.log(jnp.sum(jnp.exp(lses - peak[None]), axis=0))
-    total_ref[...] = log_total
+    log_total = total_ref[...]
     resp_ref[...] = jnp.exp(table_ref[...] - log_total[None])
     diagonal = eye_mask(width)
     identity = jnp.where(diagonal, 1.0, 0.0)
@@ -197,29 +408,39 @@
     lax.fori_loop(0, members, emit, 0)
 
 
-def first_kernel(x_ref, mu_ref, p_ref, w_ref, xt_ref, table_ref, lse_ref):
-    total, width = x_ref.shape
+def first_kernel(
+    counts_ref, dest_ref, points_ref, mu_ref, p_ref, w_ref,
+    xt_ref, table_ref, total_ref, x_ref, lse_ref, *scratch,
+):
+    greet()
+    gather_stage(counts_ref, dest_ref, points_ref, x_ref, *scratch[:12])
+    width, total = xt_ref.shape
+    flat = x_ref.reshape(total, width)
     chunk = math.gcd(total, 512)
 
     def flip(c, carry):
         at = pl.ds(pl.multiple_of(c * chunk, chunk), chunk)
-        xt_ref[:, at] = x_ref[at, :].T
+        xt_ref[:, at] = flat[at, :].T
         return carry
 
     lax.fori_loop(0, total // chunk, flip, 0)
     density_stage(xt_ref, mu_ref, p_ref, w_ref, table_ref, lse_ref)
+    merge_stage(lse_ref, total_ref, *scratch[12:])
 
 
 def middle_kernel(
-    total_points, xt_ref, table_ref, all_ref, mu_ref,
-    new_mu_ref, new_p_ref, new_w_ref, new_table_ref, lse_ref,
-    total_ref, resp_ref, m_ref, l_ref,
+    total_points, xt_ref, table_ref, total_ref, mu_ref,
+    new_mu_ref, new_p_ref, new_w_ref, new_table_ref, new_total_ref,
+    lse_ref, resp_ref, m_ref, l_ref, *scratch,
 ):
+    greet()
     update_stage(
-        total_points, xt_ref, table_ref, all_ref, mu_ref,
-        new_mu_ref, new_p_ref, new_w_ref, total_ref, resp_ref, m_ref, l_ref,
+        total_points, xt_ref, table_ref, total_ref, mu_ref,
+        new_mu_ref, new_p_ref, new_w_ref, resp_ref, m_ref, l_ref,
     )
     density_stage(xt_ref, new_mu_ref, new_p_ref, new_w_ref, new_table_ref, lse_ref)
+    greeted()
+    merge_stage(lse_ref, new_total_ref, *scratch)
 
 
 def last_kernel(total_points, *refs):
@@ -230,56 +451,50 @@
     return jax.ShapeDtypeStruct(shape, jnp.float32)
 
 
-def call(kernel, out_shape, *args, scratch=(), specs=None):
+def call(kernel, out_shape, *args, scratch=(), specs=None, params=PARAMS):
     return pl.pallas_call(
         kernel,
         out_shape=out_shape,
         in_specs=specs or [VMEM] * len(args),
         out_specs=jax.tree.map(lambda _: VMEM, out_shape),
         scratch_shapes=list(scratch),
-        compiler_params=PARAMS,
+        compiler_params=params,
     )(*args)
 
 
-def gather_live(points, block_counts, block_dest):
-    devices = lax.axis_size("dp")
-    nblocks = block_dest.shape[1]
-    width = points.shape[1]
-    rows = points.shape[0] // nblocks
-    slots = (nblocks + devices - 1) // devices
-    me = lax.axis_index("dp").astype(jnp.int32).reshape(1)
-    specs = [SMEM, SMEM, SMEM, VMEM]
-    outgoing = call(
-        pack_kernel, f32(devices * slots, rows, width),
-        me, block_counts, block_dest, points.reshape(nblocks, rows, width),
-        specs=specs, scratch=[pltpu.SMEM((devices,), jnp.int32)],
-    )
-    incoming = lax.all_to_all(outgoing, "dp", split_axis=0, concat_axis=0, tiled=True)
-    live = call(
-        order_kernel, f32(RB, rows, width), me, block_counts, block_dest, incoming, specs=specs
-    )
-    return live.reshape(RB * rows, width)
-
-
 RB = 4
-
-
-def exchange(lse):
-    return lax.all_gather(lse, ("dp", "comp"))
 
 
 def per_device(points, block_counts, block_dest, means, factors, log_weights):
     members, width = means.shape
-    mine = gather_live(points, block_counts, block_dest)
-    x = lax.all_gather(mine, "dp", axis=0, tiled=True)
-    total = x.shape[0]
-    total_points = float(total + members * lax.axis_size("dp") * lax.axis_size("comp"))
+    groups = lax.axis_size("dp")
+    comps = lax.axis_size("comp")
+    nblocks = block_dest.shape[1]
+    rows = points.shape[0] // nblocks
+    slots = (nblocks + groups - 1) // groups
+    share = rows // comps
+    total = groups * RB * rows
+    total_points = float(total + members * groups * comps)
     mu = means.reshape(members, width, 1)
     weights = log_weights.reshape(members, 1, 1)
-    factor = factors
-    xt, table, lse = call(
+    dma = pltpu.SemaphoreType.DMA
+    levels = comps.bit_length() - 1
+    gather_scratch = [
+        pltpu.VMEM((nblocks, share, width), jnp.float32),
+        pltpu.VMEM((groups, slots, share, width), jnp.float32),
+        pltpu.VMEM((groups, slots, share, width), jnp.float32),
+        pltpu.VMEM((RB, share, width), jnp.float32),
+        dma, dma((groups,)), dma((groups,)), dma((groups,)), dma((groups,)),
+        dma((levels, comps // 2, groups)), dma((levels, comps // 2, groups)), dma,
+    ]
+    x_scratch = pltpu.VMEM((groups, RB, comps, share, width), jnp.float32)
+    lse_scratch = pltpu.VMEM((1, total), jnp.float32)
+    xt, table, log_total = call(
         first_kernel, (f32(width, total), f32(members, 1, total), f32(1, total)),
-        x, mu, factor, weights,
+        block_counts, block_dest, points.reshape(nblocks, rows, width), mu, factors, weights,
+        specs=[SMEM, SMEM, ANY, VMEM, VMEM, VMEM],
+        scratch=[x_scratch, lse_scratch] + gather_scratch + merge_scratch(total),
+        params=talking(0),
     )
     scratch = [
         pltpu.VMEM((members, 1, total), jnp.float32),
@@ -287,24 +502,21 @@
         pltpu.VMEM((width * 8, width), jnp.float32),
     ]
     params = (f32(members, width, 1), f32(members, width, width), f32(members, 1, 1))
-    for iteration in range(ITERS):
-        gathered = exchange(lse)
-        if iteration < ITERS - 1:
-            mu, factor, weights, table, lse = call(
-                lambda *refs: middle_kernel(total_points, *refs),
-                params + (f32(members, 1, total), f32(1, total)),
-                xt, table, gathered, mu,
-                scratch=[pltpu.VMEM((1, total), jnp.float32)] + scratch,
-            )
-        else:
-            mu, factor, weights, log_total = call(
-                lambda *refs: last_kernel(total_points, *refs),
-                params + (f32(1, total),),
-                xt, table, gathered, mu, scratch=scratch,
-            )
-    share = total // lax.axis_size("dp")
-    own = lax.dynamic_slice_in_dim(log_total.reshape(total), lax.axis_index("dp") * share, share)
-    return (mu.reshape(members, width), factor, weights.reshape(members), own / width)
+    for iteration in range(ITERS - 1):
+        mu, factor, weights, table, log_total = call(
+            lambda *refs: middle_kernel(total_points, *refs),
+            params + (f32(members, 1, total), f32(1, total)),
+            xt, table, log_total, mu,
+            scratch=[lse_scratch] + scratch + merge_scratch(total),
+            params=talking(1 + iteration),
+        )
+    mu, factor, weights = call(
+        lambda *refs: last_kernel(total_points, *refs),
+        params, xt, table, log_total, mu, scratch=scratch,
+    )
+    own = total // groups
+    mine = lax.dynamic_slice_in_dim(log_total.reshape(total), lax.axis_index("dp") * own, own)
+    return (mu.reshape(members, width), factor, weights.reshape(members), mine / width)
 
 
 def solution(mesh):

time: 265 us -> 145 us (0.55)
  blocking collectives: 105 us -> 0 us
  waiting for transfers between devices: 37.1 us -> 0 us
  Pallas kernels: 103 us -> 137 us
  between operations: 14 us -> 0.65 us
    all_gather x2 -> x0, blocking collectives: 83 us -> none  [exchange(): return lax.all_gather(lse, ('dp', 'comp'))]
    all_gather x1 -> x0, waiting for transfers between devices: 37.1 us -> none  [per_device(): x = lax.all_gather(mine, 'dp', axis=0, tiled=True)]
    pallas_call x5 -> x3, Pallas kernels: 103 us -> 137 us  [call(): pl.pallas_call(kernel, out_shape=out_shape, in_specs=specs or [VMEM] * le...]
    all_to_all x1 -> x0, blocking collectives: 22 us -> none  [gather_live(): lax.all_to_all(outgoing, 'dp', split_axis=0, concat_axis=0, tiled=True)]
  transfers between devices with their start and end apart: 1 -> 0, of which waited for: 1 -> 0; matrix products, arithmetic and copies ran while one was open for 1% -> 0% of each run, Pallas kernels for 0% -> 0%
where the time goes in v1:
time: 145 us
  Pallas kernels  137 us (94%)
  other arithmetic  3.74 us (3%)
  local copies, waits for them, and re-layouts  3.04 us (2%)
    pallas_call x3, Pallas kernels, call(): pl.pallas_call(kernel, out_shape=out_shape, in_specs=specs or [VMEM] * le...  137 us

profile of v1, /device:TPU:0, one launch (start us, length us, event | category | flops | bytes accessed | tf_op | source)
XLA Modules:
  0.0 144.7 jit_solution(3029053758402346736)
XLA Ops:
  0.6 1.7 %copy.11.mu_ref.refs_3_ = f32[8,128,1]{2,1,0:T(8,128)} copy(f32[8,128,1]{1,0,2:T(8,128)} %bitcast.5) | data formatting | bytes 8192 | tf_op jit(solution)/shard_map/reshape | solution.py:478
  2.3 0.0 copy-start.1
  2.3 0.7 copy-done.1
  3.0 0.7 copy.12.w_ref
  3.7 47.8 %shard_map.93 = (f32[128,2048]{1,0:T(8,128)}, f32[8,1,2048]{2,1,0:T(1,128)}, f32[1,2048]{1,0:T(1,128)}) custom-call(s32[8]{0:T(128)} %counts_ref.1, s32[8,16]{1,0:T(8,128)} %dest_ref.1, f32[16,64,128]{2,1,0:T(8,128)} %bitcast.4, f32[8,128,1]{2,1,0:T(8,128)} %copy.11.mu_ref.refs_3_, f32[8,128,128]{2,1,0:T(8,128)} %p_ref.1, f32[8,1,1]{2,1,0:T(1,128)} %copy.12.w_ref), custom_call_target="tpu_custom_call" | custom-call | tf_op jit(solution)/shard_map/pallas_call | solution.py:455
  51.5 54.6 %shard_map.94 = (f32[8,128,1]{2,1,0:T(8,128)}, f32[8,128,128]{2,1,0:T(8,128)}, f32[8,1,1]{2,1,0:T(1,128)}, f32[8,1,2048]{2,1,0:T(1,128)}, f32[1,2048]{1,0:T(1,128)}) custom-call(f32[128,2048]{1,0:T(8,128)} %get-tuple-element.13.refs_0_, f32[8,1,2048]{2,1,0:T(1,128)} %get-tuple-element.14.refs_1_, f32[1,2048]{1,0:T(1,128)} %get-tuple-element.15.refs_2_, ...), custom_call_target="tpu_custom_call" | custom-call | tf_op jit(solution)/shard_map/pallas_call | solution.py:455
  106.1 34.9 %shard_map.95 = (f32[8,128,1]{2,1,0:T(8,128)}, f32[8,128,128]{2,1,0:T(8,128)}, f32[8,1,1]{2,1,0:T(1,128)}) custom-call(f32[128,2048]{1,0:T(8,128)} %get-tuple-element.13.refs_0_, f32[8,1,2048]{2,1,0:T(1,128)} %get-tuple-element.16.refs_1_, f32[1,2048]{1,0:T(1,128)} %get-tuple-element.17.refs_2_, f32[8,128,1]{2,1,0:T(8,128)} %get-tuple-element.18.refs_3_), custom_call_target="tpu_custom_call" | custom-call | tf_op jit(solution)/shard_map/pallas_call | solution.py:455
  140.9 0.0 copy-start
  140.9 1.8 %reduce = f32[8,128]{1,0:T(8,128)} reduce(f32[8,128,1]{2,1,0:T(8,128)} %get-tuple-element.19, f32[]{:T(128)} %constant.19), dimensions={2}, to_apply=%get-tuple-element.19.reduce_sub_computation | reduce | bytes 8196 | tf_op jit(solution)/shard_map/pallas_call | solution.py:455
  142.8 0.0 copy-done
  142.8 0.7 reduce.1
  143.4 1.2 dynamic-slice_multiply_fusion
Async XLA Ops:
  2.3 0.7 copy-start.1
  140.9 1.8 %copy-start = (f32[8,1,1]{2,1,0:T(1,128)S(1)}, f32[8,1,1]{2,1,0:T(1,128)}, u32[]{:S(2)}) copy-start(f32[8,1,1]{2,1,0:T(1,128)} %get-tuple-element.21) | copy-start | bytes 100
